TPU v7x, 32 devices: a whole 2x2x4 slice. The times are simulated.
32 devices in a mesh: shard: 4 (over z), ctx: 4 (over y, x), tp: 2 (over core).
Axes of the slice: x: 2, y: 2, z: 4, core: 2. Of those that a mesh axis runs over, the one named last changes fastest.
Arguments:
- hidden_in: bfloat16 [4, 512, 1536], P('shard', 'ctx'), may hold values from -6 to 6
- seg_start: int32 [4, 512], P('shard', 'ctx'), may hold values from 0 to 511, as said below
- norm1_gain: bfloat16 [1536], P('shard'), may hold values from 0.5 to 1.5
- w_qkv: bfloat16 [1536, 2, 8, 128], P('shard', 'tp'), may hold values from -0.15625 to 0.15625
- b_qkv: bfloat16 [128, 2, 8], P('shard', 'tp'), may hold values from -2 to 2
- w_attn_out: bfloat16 [1536, 1536], P('shard', 'tp'), may hold values from -0.875 to 0.875
- norm2_gain: bfloat16 [1536], P('shard'), may hold values from 0.5 to 1.5
- w_gate_up: bfloat16 [1536, 2, 8960], P('shard', None, 'tp'), may hold values from -0.15625 to 0.15625
- w_down: bfloat16 [1536, 8960], P('shard', 'tp'), may hold values from -0.0625 to 0.0625
- out_grad: bfloat16 [4, 512, 1536], P('shard', 'ctx'), may hold values from -6 to 6
Outputs:
- layer_out: float32 [4, 512, 1536], P('shard', 'ctx')
- in_grad: float32 [4, 512, 1536], P('shard', 'ctx')
- grad_norm1: float32 [1536], P('shard')
- grad_qkv: float32 [1536, 2, 8, 128], P('shard', 'tp')
- grad_bias: float32 [128, 2, 8], P('shard', 'tp')
- grad_attn_out: float32 [1536, 1536], P('shard', 'tp')
- grad_norm2: float32 [1536], P('shard')
- grad_gate_up: float32 [1536, 2, 8960], P('shard', None, 'tp')
- grad_down: float32 [1536, 8960], P('shard', 'tp')
Inputs may be any that keep to these rules, and one draw needn't show every extreme that they name: seg_start never falls along a row and equals its own position at a segment's first token; every segment holds 1 to 256 tokens, and every row has a segment of exactly 256 tokens.
All inputs are finite; a program needn't handle non-finite values.
Results may differ from a plain program's by a relative error of at most 0.02.
Values may be sent and summed in bfloat16 or wider, within the bound.
A program may use at most 320 MiB of HBM per device.

v0:
```python
import jax
import jax.numpy as jnp
from jax import lax
from jax.sharding import PartitionSpec as P

EPSILON = 1e-06
ROPE_BASE = 1000000.0
NEGATIVE = -1e30


def rope_tables(positions, head_dim):
    half_dim = head_dim // 2
    frequency = ROPE_BASE ** (-(jnp.arange(half_dim, dtype=jnp.float32) * 2.0) / head_dim)
    angles = positions[:, None] * frequency[None, :]
    cosine = jnp.cos(angles)
    sine_vals = jnp.sin(angles)
    return (jnp.concatenate([cosine, cosine], -1), jnp.concatenate([sine_vals, sine_vals], -1))


def rotate_half(values):
    half_dim = values.shape[-1] // 2
    return jnp.concatenate([-values[..., half_dim:], values[..., :half_dim]], -1)


def rotate_back(values):
    half_dim = values.shape[-1] // 2
    return jnp.concatenate([values[..., half_dim:], -values[..., :half_dim]], -1)


def apply_rope(values, cosine, sine_vals):
    return values * cosine + rotate_half(values) * sine_vals


def rope_grad(grads, cosine, sine_vals):
    return grads * cosine + rotate_back(grads * sine_vals)


def rms_back(grad_norm, inputs, inv_rms, gain_vals):
    scaled = gain_vals * grad_norm
    return inv_rms * scaled - inputs * (inv_rms * inv_rms * inv_rms) * jnp.mean(
        scaled * inputs, -1, keepdims=True
    )


def tensor_sum(partial_sum):
    return lax.psum(partial_sum, "tp")


def contract_rows(left, right):
    return lax.dot_general(
        left, right, (((0,), (0,)), ((), ())), preferred_element_type=jnp.float32
    )


def contract_cols(left, right):
    return lax.dot_general(
        left, right, (((1,), (1,)), ((), ())), preferred_element_type=jnp.float32
    )


def body(
    hidden_in,
    seg_start,
    norm1_gain,
    w_qkv,
    b_qkv,
    w_attn_out,
    norm2_gain,
    w_gate_up,
    w_down,
    out_grad,
):
    shards = lax.axis_size("shard")
    ctxs = lax.axis_size("ctx")
    ctx_id = lax.axis_index("ctx")
    tp_id = lax.axis_index("tp")
    everyone = ("shard", "ctx", "tp")
    bf16 = jnp.bfloat16
    qkv_full, attn_out_full, gain_one_bf, bias_full, gain_two_bf = (
        lax.all_gather(w_qkv, "shard", axis=0, tiled=True),
        lax.all_gather(w_attn_out, "shard", axis=0, tiled=True),
        lax.all_gather(norm1_gain, "shard", axis=0, tiled=True),
        lax.all_gather(b_qkv, "shard", axis=0, tiled=True),
        lax.all_gather(norm2_gain, "shard", axis=0, tiled=True),
    )
    tokens, width = (hidden_in.shape[1], hidden_in.shape[2])
    half = tokens // lax.axis_size("tp")
    part = w_gate_up.shape[0]
    hidden_units = w_down.shape[1] // (shards * ctxs)

    def my_units(weights):
        blocks = weights.reshape(weights.shape[:-1] + (ctxs, shards * hidden_units))
        return lax.dynamic_index_in_dim(blocks, ctx_id, weights.ndim - 1, keepdims=False)

    def my_half(rows):
        return lax.dynamic_slice_in_dim(rows, tp_id * half, half, 0)

    mine = jnp.concatenate([my_units(w_gate_up), my_units(w_down)[:, None]], 1)
    mine = jnp.transpose(mine.reshape(part, 3, shards, hidden_units), (2, 0, 1, 3))
    units = lax.all_to_all(mine, "shard", split_axis=0, concat_axis=0, tiled=True)
    units = units.reshape(shards * part, 3, hidden_units)
    gate_up_w = units[:, :2].reshape(shards * part, 2 * hidden_units)
    down_w = units[:, 2]
    grad_rows = out_grad[0]
    grad_all = lax.all_gather(my_half(grad_rows), everyone, axis=0, tiled=True)
    kv_local = qkv_full.shape[1]
    head_dim = qkv_full.shape[3]
    groups = qkv_full.shape[2] - 2
    query_scale = head_dim ** (-0.5)
    grad_scale = float(shards * ctxs * tokens) ** (-0.5)
    gain_one = gain_one_bf.astype(jnp.float32)
    gain_two = gain_two_bf.astype(jnp.float32)
    bias_vals = jnp.transpose(bias_full.astype(jnp.float32), (1, 2, 0))
    inputs = hidden_in[0].astype(jnp.float32)
    seg_row = seg_start[0]
    token_ids = ctx_id * tokens + jnp.arange(tokens, dtype=jnp.int32)
    cosine, sine_vals = rope_tables((token_ids - seg_row).astype(jnp.float32), head_dim)
    cos_four = cosine[:, None, None, :]
    sin_four = sine_vals[:, None, None, :]
    cos_three = cosine[:, None, :]
    sin_three = sine_vals[:, None, :]
    inv_rms1 = lax.rsqrt(jnp.mean(inputs * inputs, -1, keepdims=True) + EPSILON)
    normed1 = (inputs * inv_rms1 * gain_one).astype(bf16)
    qkv_vals = (
        jnp.einsum("td,dcsh->tcsh", normed1, qkv_full, preferred_element_type=jnp.float32)
        + bias_vals
    )
    q_rot = (apply_rope(qkv_vals[:, :, :groups], cos_four, sin_four) * query_scale).astype(bf16)
    k_rot = apply_rope(qkv_vals[:, :, groups], cos_three, sin_three).astype(bf16)
    v_vals = qkv_vals[:, :, groups + 1].astype(bf16)
    query_heads = jnp.transpose(q_rot, (1, 2, 0, 3))
    key_value = jnp.stack([k_rot, v_vals], axis=2)
    key_value = lax.all_gather(key_value, "ctx", axis=0, tiled=True)
    keys, values = (key_value[:, :, 0], key_value[:, :, 1])
    length = keys.shape[0]
    key_ids = jnp.arange(length, dtype=jnp.int32)
    allowed = (key_ids[None, :] <= token_ids[:, None]) & (key_ids[None, :] >= seg_row[:, None])
    scores = jnp.einsum("cgqh,kch->cgqk", query_heads, keys, preferred_element_type=jnp.float32)
    scores = jnp.where(allowed, scores, NEGATIVE)
    top_all = jnp.max(scores, -1, keepdims=True)
    raised = jnp.where(allowed, jnp.exp(scores - top_all), 0.0)
    total_all = jnp.sum(raised, -1, keepdims=True)
    attn_probs = raised / total_all
    probs_bf = attn_probs.astype(bf16)
    attn_vals = jnp.einsum(
        "cgqk,kch->cgqh", probs_bf, values, preferred_element_type=jnp.float32
    ).astype(bf16)
    attn_flat = jnp.transpose(attn_vals, (2, 0, 1, 3)).reshape(tokens, kv_local * groups * head_dim)
    resid1 = inputs + tensor_sum(contract_cols(attn_flat, attn_out_full))
    inv_rms2 = lax.rsqrt(jnp.mean(resid1 * resid1, -1, keepdims=True) + EPSILON)
    normed2 = (resid1 * inv_rms2 * gain_two).astype(bf16)
    normed2_all = lax.all_gather(my_half(normed2), everyone, axis=0, tiled=True)
    gate_up = jnp.dot(normed2_all, gate_up_w, preferred_element_type=jnp.float32)
    gate_vals, up_vals = (gate_up[:, :hidden_units], gate_up[:, hidden_units:])
    sigmoid_gate = jax.nn.sigmoid(gate_vals)
    silu_gate = gate_vals * sigmoid_gate
    hidden_act = (silu_gate * up_vals).astype(bf16)
    d_hidden = jnp.dot(grad_all, down_w, preferred_element_type=jnp.float32)
    d_gate = d_hidden * up_vals * sigmoid_gate * (1.0 + gate_vals * (1.0 - sigmoid_gate))
    d_up = d_hidden * silu_gate
    d_gate_up = jnp.concatenate([d_gate, d_up], 1).astype(bf16)

    def scatter_sum(partial_sum):
        share = lax.psum_scatter(
            partial_sum.astype(bf16), everyone, scatter_dimension=0, tiled=True
        )
        return lax.all_gather(share, "tp", axis=0, tiled=True).astype(jnp.float32)

    d_normed2 = scatter_sum(contract_cols(d_gate_up, gate_up_w))
    layer_out = resid1 + scatter_sum(contract_cols(hidden_act, down_w))
    grad_down = contract_rows(grad_all, hidden_act).astype(bf16)
    grad_gate_up = contract_rows(normed2_all, d_gate_up).astype(bf16)
    made = jnp.concatenate([grad_gate_up, grad_down], 1).reshape(shards, part, 3 * hidden_units)
    made = lax.all_to_all(made, "shard", split_axis=0, concat_axis=0, tiled=True)
    made = lax.all_gather(made, "ctx", axis=0, tiled=False)
    made = made.reshape(ctxs, shards, part, 3, hidden_units)
    made = jnp.transpose(made, (2, 3, 0, 1, 4)).reshape(part, 3, ctxs * shards * hidden_units)
    made = made.astype(jnp.float32) * grad_scale
    grad_norm2 = jnp.sum(d_normed2 * resid1 * inv_rms2, 0)
    d_resid1 = grad_rows.astype(jnp.float32) + rms_back(d_normed2, resid1, inv_rms2, gain_two)
    d_resid1_bf = d_resid1.astype(bf16)
    d_attn_flat = jnp.dot(d_resid1_bf, attn_out_full, preferred_element_type=jnp.float32)
    grad_attn_out = contract_rows(d_resid1_bf, attn_flat)
    d_attn = jnp.transpose(d_attn_flat.reshape(tokens, kv_local, groups, head_dim), (1, 2, 0, 3))
    delta_vals = jnp.sum(d_attn * attn_vals.astype(jnp.float32), -1)
    d_attn_bf = d_attn.astype(bf16)
    d_value = jnp.einsum("cgqk,cgqh->kch", probs_bf, d_attn_bf, preferred_element_type=jnp.float32)
    d_probs = jnp.einsum("cgqh,kch->cgqk", d_attn_bf, values, preferred_element_type=jnp.float32)
    d_scores = (attn_probs * (d_probs - delta_vals[..., None])).astype(bf16)
    d_query = jnp.einsum("cgqk,kch->cgqh", d_scores, keys, preferred_element_type=jnp.float32)
    d_key = jnp.einsum("cgqk,cgqh->kch", d_scores, query_heads, preferred_element_type=jnp.float32)
    key_grads = lax.psum_scatter(
        jnp.stack([d_key, d_value], 2).astype(bf16), "ctx", scatter_dimension=0, tiled=True
    ).astype(jnp.float32)
    d_query_rows = jnp.transpose(d_query, (2, 0, 1, 3))
    d_qkv = jnp.concatenate(
        [
            rope_grad(d_query_rows, cos_four, sin_four) * query_scale,
            rope_grad(key_grads[:, :, 0], cos_three, sin_three)[:, :, None],
            key_grads[:, :, 1][:, :, None],
        ],
        2,
    )
    grad_bias = jnp.transpose(jnp.sum(d_qkv, 0), (2, 0, 1))
    d_qkv_bf = d_qkv.astype(bf16)
    grad_qkv = jnp.einsum("td,tcsh->dcsh", normed1, d_qkv_bf, preferred_element_type=jnp.float32)
    d_normed1 = tensor_sum(
        jnp.einsum("tcsh,dcsh->td", d_qkv_bf, qkv_full, preferred_element_type=jnp.float32)
    )
    grad_norm1 = jnp.sum(d_normed1 * inputs * inv_rms1, 0)
    in_grad = d_resid1 + rms_back(d_normed1, inputs, inv_rms1, gain_one)

    def total(partial_sum):
        share = lax.psum_scatter(partial_sum.astype(bf16), "shard", scatter_dimension=0, tiled=True)
        return lax.psum(share, "ctx").astype(jnp.float32) * grad_scale

    return (
        layer_out[None],
        in_grad[None],
        total(grad_norm1),
        total(grad_qkv),
        total(grad_bias),
        total(grad_attn_out),
        total(grad_norm2),
        made[:, :2],
        made[:, 2],
    )


def solution(mesh):
    in_specs = (
        P("shard", "ctx", None),
        P("shard", "ctx"),
        P("shard"),
        P("shard", "tp", None, None),
        P("shard", "tp", None),
        P("shard", "tp"),
        P("shard"),
        P("shard", None, "tp"),
        P("shard", "tp"),
        P("shard", "ctx", None),
    )
    out_specs = (
        P("shard", "ctx", None),
        P("shard", "ctx", None),
        P("shard"),
        P("shard", "tp", None, None),
        P("shard", "tp", None),
        P("shard", "tp"),
        P("shard"),
        P("shard", None, "tp"),
        P("shard", "tp"),
    )
    return jax.shard_map(body, mesh=mesh, in_specs=in_specs, out_specs=out_specs, check_vma=False)
```

profile of v0, /device:TPU:0, one launch (start us, length us, event | category | flops | bytes accessed | tf_op | source)
XLA Modules:
  0.0 1046.7 jit_solution(12587943593719788081)
XLA Ops:
  10.6 13.6 %all-gather.2 = bf16[4,1,384]{2,1,0:T(2,128)(2,1)S(1)} all-gather(bf16[1,1,384]{2,1,0:T(2,128)(2,1)S(1)} %reshape.562), channel_id=1, replica_groups=mesh['shard'=4,'ctx'=4,'tp'=2] {'shard'}, dimensions={0}, use_global_device_ids=true | all-gather | bytes 3840 | tf_op jit(solution)/shard_map/all_gather | solution.py:82
  25.2 15.2 %all_gather.38 = bf16[128,1,8]{2,1,0:T(2,128)(2,1)S(1)} all-gather(bf16[32,1,8]{2,1,0:T(2,128)(2,1)S(1)} %copy.68), channel_id=1, replica_groups=mesh['shard'=4,'ctx'=4,'tp'=2] {'shard'}, dimensions={0}, use_global_device_ids=true | all-gather | bytes 2560 | tf_op jit(solution)/shard_map/all_gather | solution.py:83
  41.7 35.5 %all-gather.10.cloned.1.call-done = bf16[1536,1,8,128]{0,3,2,1:T(8,128)(2,1)} async-done(((bf16[384,1,8,128]{0,3,2,1:T(8,128)(2,1)}), bf16[1536,1,8,128]{0,3,2,1:T(8,128)(2,1)}) %all-gather.10.cloned.1.call-update) | async-done | bytes 3145744 | tf_op jit(solution)/shard_map/all_gather | solution.py:80
  80.4 8.9 all_gather.39
  90.9 36.5 %all-gather.12.cloned.1.call-done = bf16[1536,768]{1,0:T(8,128)(2,1)} async-done(((bf16[384,768]{1,0:T(8,128)(2,1)}), bf16[1536,768]{1,0:T(8,128)(2,1)}) %all-gather.12.cloned.1.call-update) | async-done | bytes 2359312 | tf_op jit(solution)/shard_map/all_gather | solution.py:81
  130.9 12.1 %all-gather.3 = bf16[4,1,384]{2,1,0:T(2,128)(2,1)S(1)} all-gather(bf16[1,1,384]{2,1,0:T(2,128)(2,1)S(1)} %reshape.564), channel_id=1, replica_groups=mesh['shard'=4,'ctx'=4,'tp'=2] {'shard'}, dimensions={0}, use_global_device_ids=true | all-gather | bytes 3840 | tf_op jit(solution)/shard_map/all_gather | solution.py:84
  158.1 18.0 %copy.72 = bf16[384,2,4480]{0,2,1:T(8,128)(2,1)} copy(bf16[384,2,4480]{2,1,0:T(2,128)(2,1)} %param.17) | data formatting | bytes 13762560 | tf_op args[7]
  179.6 85.7 %all_to_all.10 = bf16[4,384,3,280]{1,3,2,0:T(8,128)(2,1)S(1)} all-to-all(bf16[4,384,3,280]{1,3,2,0:T(8,128)(2,1)S(1)} %copy.74), channel_id=1, replica_groups=mesh['shard'=4,'ctx'=4,'tp'=2] {'shard'}, dimensions={0} | all-to-all | bytes 5160960 | tf_op jit(solution)/shard_map/all_to_all | solution.py:100
  268.4 9.2 fusion.91
  277.5 42.8 %all-gather.16.cloned.1.call-done = bf16[1,2048,1536]{2,1,0:T(8,128)(2,1)} async-done(((bf16[1,64,1536]{2,1,0:T(8,128)(2,1)}), bf16[1,2048,1536]{2,1,0:T(8,128)(2,1)}) %all-gather.16.cloned.1.call-update) | async-done | bytes 6291472 | tf_op jit(solution)/shard_map/all_gather | solution.py:105
  344.7 105.9 %reduce-scatter.13.cloned.1.call-done = bf16[64,1536]{1,0:T(8,128)(2,1)} async-done(((bf16[2048,1536]{1,0:T(8,128)(2,1)}), bf16[64,1536]{1,0:T(8,128)(2,1)}) %reduce-scatter.13.cloned.1.call-update) | async-done | bytes 196624 | tf_op jit(solution)/shard_map/reduce_scatter | solution.py:164
  454.2 116.5 %reduce-scatter.11.cloned.1.call-done = bf16[64,1536]{1,0:T(8,128)(2,1)} async-done(((bf16[2048,1536]{1,0:T(8,128)(2,1)}), bf16[64,1536]{1,0:T(8,128)(2,1)}) %reduce-scatter.11.cloned.1.call-update) | async-done | bytes 196624 | tf_op jit(solution)/shard_map/reduce_scatter | solution.py:164
  584.5 19.4 %reduce-scatter.19.cloned.1.call-done = bf16[128,256]{1,0:T(8,128)(2,1)} async-done(((bf16[512,256]{1,0:T(8,128)(2,1)}), bf16[128,256]{1,0:T(8,128)(2,1)}) %reduce-scatter.19.cloned.1.call-update) | async-done | bytes 65552
  634.2 43.2 %reduce-scatter.17.cloned.1.call-done = bf16[384,768]{1,0:T(8,128)(2,1)} async-done(((bf16[1536,768]{1,0:T(8,128)(2,1)}), bf16[384,768]{1,0:T(8,128)(2,1)}) %reduce-scatter.17.cloned.1.call-update) | async-done | bytes 589840 | tf_op jit(solution)/shard_map/reduce_scatter | solution.py:214
  677.4 82.8 %reduce-scatter.15.cloned.1.call-done = bf16[384,1,8,128]{3,0,2,1:T(8,128)(2,1)} async-done(((bf16[1536,1,8,128]{3,0,2,1:T(8,128)(2,1)}), bf16[384,1,8,128]{3,0,2,1:T(8,128)(2,1)}) %reduce-scatter.15.cloned.1.call-update) | async-done | bytes 786448 | tf_op jit(solution)/shard_map/reduce_scatter | solution.py:214
  762.0 19.3 %reduce-scatter.21.cloned.1.call-done = bf16[32,8]{1,0:T(8,128)(2,1)} async-done(((bf16[128,8]{1,0:T(8,128)(2,1)}), bf16[32,8]{1,0:T(8,128)(2,1)}) %reduce-scatter.21.cloned.1.call-update) | async-done | bytes 528
  782.1 19.1 %all-reduce.11.cloned.1.call-done = f32[128,1536]{1,0:T(8,128)} async-done(((f32[128,1536]{1,0:T(8,128)}), f32[128,1536]{1,0:T(8,128)}) %all-reduce.11.cloned.1.call-update) | async-done | bytes 786448 | tf_op jit(solution)/shard_map/psum | solution.py:46
  802.6 12.2 %all-reduce.4 = (bf16[1536]{0:T(1024)(128)(2,1)S(1)}, bf16[1536]{0:T(1024)(128)(2,1)S(1)}) all-reduce(bf16[1536]{0:T(1024)(128)(2,1)S(1)} %get-tuple-element.47, bf16[1536]{0:T(1024)(128)(2,1)S(1)} %copy-done.24), channel_id=7, replica_groups=mesh['shard'=4,'ctx'=4,'tp'=2] {'shard'}, use_global_device_ids=true, to_apply=%region_13.14.clone | all-reduce | flops 3072 | bytes 12288
  814.9 10.1 all-reduce.2
  829.1 34.2 %all-reduce.13.cloned.1.call-done = (bf16[384,1,8,128]{3,0,2,1:T(8,128)(2,1)}, bf16[384,768]{1,0:T(8,128)(2,1)}) async-done(((bf16[384,1,8,128]{3,0,2,1:T(8,128)(2,1)}, bf16[384,768]{1,0:T(8,128)(2,1)}), (bf16[384,1,8,128]{3,0,2,1:T(8,128)(2,1)}, bf16[384,768]{1,0:T(8,128)(2,1)})) %all-reduce.13.cloned.1.call-update) | async-done | bytes 1376272 | tf_op jit(solution)/shard_map/psum | solution.py:215
  867.8 100.8 %all-gather.18.cloned.1.call-done = bf16[16,384,840]{1,2,0:T(8,128)(2,1)} async-done(((bf16[4,384,840]{1,2,0:T(8,128)(2,1)}), bf16[16,384,840]{1,2,0:T(8,128)(2,1)}) %all-gather.18.cloned.1.call-update) | async-done | bytes 10321936 | tf_op jit(solution)/shard_map/all_gather | solution.py:175
  968.6 12.6 %convert_multiply_fusion = f32[16,384,840]{1,2,0:T(8,128)} fusion(bf16[16,384,840]{1,2,0:T(8,128)(2,1)} %all-gather.18.cloned.1.call-done), kind=kLoop, calls=%fused_computation.1 | loop fusion | flops 10321920 | bytes 30965760 | tf_op jit(solution)/shard_map/mul | solution.py:178
  999.5 10.7 %slice.106 = f32[384,2,4480]{0,2,1:T(8,128)} slice(f32[384,3,4480]{0,2,1:T(8,128)} %bitcast.226), slice={[0:384], [0:2], [0:4480]} | slice | bytes 27525120 | tf_op jit(solution)/shard_map/slice | solution.py:225
  1010.2 21.5 %copy.86 = f32[384,2,4480]{2,1,0:T(2,128)} copy(f32[384,2,4480]{0,2,1:T(8,128)} %slice.106) | data formatting | bytes 27525120
  (209 shorter events, 145.7 us)
Async XLA Ops:
  7.2 69.9 %all-gather.10.cloned.1.call-start = ((), (), s32[]{:S(2)}) async-start(), calls=%async_computation.8 | async-start | bytes 3932160 | tf_op jit(solution)/shard_map/all_gather | solution.py:80
  9.8 117.6 %all-gather.12.cloned.1.call-start = ((), (), s32[]{:S(2)}) async-start(), calls=%async_computation.9 | async-start | bytes 2949120 | tf_op jit(solution)/shard_map/all_gather | solution.py:81
  10.5 138.2 %all-reduce.9.cloned.1.call-start = ((), (), s32[]{:S(2)}) async-start(), calls=%async_computation.10 | async-start | bytes 1572864 | tf_op jit(solution)/shard_map/psum | solution.py:46
  25.1 64.2 %copy-start.14 = (f32[128,128]{0,1:T(8,128)}, f32[128,128]{0,1:T(8,128)S(1)}, u32[]{:S(2)}) copy-start(f32[128,128]{0,1:T(8,128)S(1)} %get-tuple-element.85) | copy-start | bytes 196612
  25.1 64.2 %copy-start.17 = (f32[128,128]{0,1:T(8,128)}, f32[128,128]{0,1:T(8,128)S(1)}, u32[]{:S(2)}) copy-start(f32[128,128]{0,1:T(8,128)S(1)} %get-tuple-element.86) | copy-start | bytes 196612
  90.3 40.5 %copy-start.8 = (f32[6,128,512]{2,1,0:T(8,128)}, f32[6,128,512]{2,1,0:T(8,128)S(1)}, u32[]{:S(2)}) copy-start(f32[6,128,512]{2,1,0:T(8,128)S(1)} %get-tuple-element.84) | copy-start | bytes 4718596
  90.5 40.4 %copy-start.32 = (bf16[384]{0:T(512)(128)(2,1)S(1)}, bf16[384]{0:T(512)(128)(2,1)}, u32[]{:S(2)}) copy-start(bf16[384]{0:T(512)(128)(2,1)} %param.16) | copy-start | bytes 2308
  130.8 137.5 %all-gather.14.cloned.1.call-start = ((), (), s32[]{:S(2)}) async-start(), calls=%async_computation.11 | async-start | bytes 6488064 | tf_op jit(solution)/shard_map/all_gather | solution.py:152
  150.5 302.3 %copy-start.29 = (f32[128]{0:T(128)}, f32[128]{0:T(128)S(1)}, u32[]{:S(2)}) copy-start(f32[128]{0:T(128)S(1)} %get-tuple-element.82) | copy-start | bytes 1540
  151.4 168.9 %all-gather.16.cloned.1.call-start = ((), (), s32[]{:S(2)}) async-start(), calls=%async_computation.17 | async-start | bytes 6488064 | tf_op jit(solution)/shard_map/all_gather | solution.py:105
  152.2 298.3 %reduce-scatter.13.cloned.1.call-start = ((), (), s32[]{:S(2)}) async-start(), calls=%async_computation.13 | async-start | bytes 6488064 | tf_op jit(solution)/shard_map/reduce_scatter | solution.py:164
  336.8 233.9 %reduce-scatter.11.cloned.1.call-start = ((), (), s32[]{:S(2)}) async-start(), calls=%async_computation.12 | async-start | bytes 6488064 | tf_op jit(solution)/shard_map/reduce_scatter | solution.py:164
  344.6 259.3 %reduce-scatter.19.cloned.1.call-start = ((), (), s32[]{:S(2)}) async-start(), calls=%async_computation.19 | async-start | bytes 327680
  580.5 97.0 %reduce-scatter.17.cloned.1.call-start = ((), (), s32[]{:S(2)}) async-start(), calls=%async_computation.16 | async-start | bytes 2949120 | tf_op jit(solution)/shard_map/reduce_scatter | solution.py:214
  582.8 177.4 %reduce-scatter.15.cloned.1.call-start = ((), (), s32[]{:S(2)}) async-start(), calls=%async_computation.15 | async-start | bytes 3932160 | tf_op jit(solution)/shard_map/reduce_scatter | solution.py:214
  624.0 136.3 %all-to-all-start.1 = ((bf16[4,384,840]{1,2,0:T(8,128)(2,1)}), bf16[4,384,840]{1,2,0:T(8,128)(2,1)}, u32[]{:S(2)}, u32[]{:S(2)}) async-start(bf16[4,384,840]{1,2,0:T(8,128)(2,1)} %bitcast.230), calls=%async_computation.5 | async-start | bytes 5160960 | tf_op jit(solution)/shard_map/all_to_all | solution.py:174
  628.8 152.5 %reduce-scatter.21.cloned.1.call-start = ((), (), s32[]{:S(2)}) async-start(), calls=%async_computation.20 | async-start | bytes 40960
  631.6 169.6 %all-reduce.11.cloned.1.call-start = ((), (), s32[]{:S(2)}) async-start(), calls=%async_computation.14 | async-start | bytes 1572864 | tf_op jit(solution)/shard_map/psum | solution.py:46
  634.1 126.7 %copy-start.35 = (u32[32]{0:T(128)S(1)}, u32[32]{0:T(128)}, u32[]{:S(2)}) copy-start(u32[32]{0:T(128)} %constant.62) | copy-start | bytes 388
  634.2 229.1 %all-reduce.13.cloned.1.call-start = ((), (), s32[]{:S(2)}) async-start(), calls=%async_computation.21 | async-start | bytes 2752512 | tf_op jit(solution)/shard_map/psum | solution.py:215
  760.2 42.4 %copy-start.24 = (bf16[1536]{0:T(1024)(128)(2,1)S(1)}, bf16[1536]{0:T(1024)(128)(2,1)}, u32[]{:S(2)}) copy-start(bf16[1536]{0:T(1024)(128)(2,1)} %get-tuple-element.45) | copy-start | bytes 9220
  760.2 66.6 %copy-start.4 = (f32[128,1536]{1,0:T(8,128)S(1)}, f32[128,1536]{1,0:T(8,128)}, u32[]{:S(2)}) copy-start(f32[128,1536]{1,0:T(8,128)} %copy-done.3) | copy-start | bytes 2359300
  760.2 66.6 %copy-start.34 = (f32[128]{0:T(128)S(1)}, f32[128]{0:T(128)}, u32[]{:S(2)}) copy-start(f32[128]{0:T(128)} %get-tuple-element.79) | copy-start | bytes 1540
  760.2 208.4 %all-gather.18.cloned.1.call-start = ((), (), s32[]{:S(2)}) async-start(), calls=%async_computation.18 | async-start | bytes 12902400 | tf_op jit(solution)/shard_map/all_gather | solution.py:175
  (32 other events, 366.2 us)
Sparse Core Ops, SparseCore 0:
  10.2 66.9 all-gather.9
  78.7 48.5 all-gather.11
  130.9 17.7 all-reduce.8
  152.0 97.6 all-gather.13
  252.9 67.3 all-gather.15
  337.0 113.5 reduce-scatter.12
  456.7 113.9 reduce-scatter.10
  580.6 23.2 reduce-scatter.18
  606.2 71.1 reduce-scatter.16
  680.1 79.9 reduce-scatter.14
  763.0 18.2 reduce-scatter.20
  784.1 17.0 all-reduce.10
  804.3 58.8 all-reduce.12
  865.0 103.5 all-gather.17
where the time goes:
time: 1050 us
  waiting for transfers between devices  663 us (63%)
  blocking collectives  162 us (15%)
  local copies, waits for them, and re-layouts  105 us (10%)
  matrix products  63.1 us (6%)
  other arithmetic  32.7 us (3%)
  between operations  15.3 us (1%)
    reduce_scatter x2, waiting for transfers between devices, scatter_sum(): lax.psum_scatter(partial_sum.astype(bf16), everyone, scatter_dimension=0,...  222 us
    reduce_scatter x2, waiting for transfers between devices, total(): lax.psum_scatter(partial_sum.astype(bf16), 'shard', scatter_dimension=0,...  126 us
    all_gather x1, waiting for transfers between devices, body(): made = lax.all_gather(made, 'ctx', axis=0, tiled=False)  101 us
    all_to_all x1, blocking collectives, body(): lax.all_to_all(mine, 'shard', split_axis=0, concat_axis=0, tiled=True)  85.7 us
    unnamed x98, local copies, waits for them, and re-layouts  74.5 us
    all_gather x1, waiting for transfers between devices, body(): grad_all = lax.all_gather(my_half(grad_rows), everyone, axis=0, tiled=True)  42.8 us
    unnamed x16, waiting for transfers between devices  40.1 us
    all_gather x1, waiting for transfers between devices, body(): lax.all_gather(w_attn_out, 'shard', axis=0, tiled=True)  36.5 us
  transfers between devices with their start and end apart: 15, of which 13 were waited for; matrix products, arithmetic and copies ran while one was open for 9% of the time, Pallas kernels for 0%

commit v1 on v0

--- a/solution.py
+++ b/solution.py
@@ -1,3 +1,4 @@
+import functools
 import jax
 import jax.numpy as jnp
 from jax import lax
@@ -6,6 +7,31 @@
 EPSILON = 1e-06
 ROPE_BASE = 1000000.0
 NEGATIVE = -1e30
+
+
+def _move_islands(matrix, axis_no):
+    near = list(matrix.shape[1:])
+    near[axis_no] *= matrix.shape[0]
+    return jnp.moveaxis(matrix, 0, axis_no).reshape(near)
+
+
+def pair_rails(u_in, chip_axis):
+    extent = lax.psum(1, chip_axis)
+    next_value = u_in[None]
+    for at in range(extent.bit_length() - 1):
+        q_next = 1 << at
+        passed = lax.ppermute(next_value, chip_axis, [(no, no ^ q_next) for no in range(extent)])
+        side_arr = jnp.stack([next_value, passed], axis=0)
+        ready = lax.axis_index(chip_axis) >> at & 1
+        next_value = jnp.where(ready == 0, side_arr, side_arr[::-1]).reshape(-1, *u_in.shape)
+    return next_value
+
+
+def link_columns(buf, tile_in, k_dim):
+    return _move_islands(pair_rails(buf, tile_in), k_dim)
+
+
+_test_spot = functools.partial(link_columns, tile_in="shard", k_dim=0)
 
 
 def rope_tables(positions, head_dim):
@@ -78,7 +104,7 @@
     bf16 = jnp.bfloat16
     qkv_full, attn_out_full, gain_one_bf, bias_full, gain_two_bf = (
         lax.all_gather(w_qkv, "shard", axis=0, tiled=True),
-        lax.all_gather(w_attn_out, "shard", axis=0, tiled=True),
+        _test_spot(w_attn_out),
         lax.all_gather(norm1_gain, "shard", axis=0, tiled=True),
         lax.all_gather(b_qkv, "shard", axis=0, tiled=True),
         lax.all_gather(norm2_gain, "shard", axis=0, tiled=True),

time: 1050 us -> 1080 us (1.029)
  blocking collectives: 162 us -> 251 us
  waiting for transfers between devices: 663 us -> 593 us
    all_gather x1, blocking collectives: 15.2 us -> 80.1 us  [body(): lax.all_gather(b_qkv, 'shard', axis=0, tiled=True)]
    all_gather x1 -> x0, waiting for transfers between devices: 36.5 us -> none  [body(): lax.all_gather(w_attn_out, 'shard', axis=0, tiled=True)]
    all_gather x1, waiting for transfers between devices: 35.5 us -> 0.02 us  [body(): lax.all_gather(w_qkv, 'shard', axis=0, tiled=True)]
    all_gather x1, blocking collectives: 13.6 us -> 37.7 us  [body(): lax.all_gather(norm1_gain, 'shard', axis=0, tiled=True)]
    unnamed x16 -> x15, waiting for transfers between devices: 40.1 us -> 40.7 us
  transfers between devices with their start and end apart: 15 -> 16, of which waited for: 13 -> 11; matrix products, arithmetic and copies ran while one was open for 9% -> 9% of each run, Pallas kernels for 0% -> 0%
where the time goes in v1:
time: 1080 us; the launch traced here: 1070 us
  waiting for transfers between devices  593 us (55%)
  blocking collectives  251 us (23%)
  local copies, waits for them, and re-layouts  108 us (10%)
  matrix products  63.8 us (6%)
  other arithmetic  33.7 us (3%)
  between operations  15.3 us (1%)
    reduce_scatter x2, waiting for transfers between devices, scatter_sum(): lax.psum_scatter(partial_sum.astype(bf16), everyone, scatter_dimension=0,...  220 us
    reduce_scatter x2, waiting for transfers between devices, total(): lax.psum_scatter(partial_sum.astype(bf16), 'shard', scatter_dimension=0,...  130 us
    all_gather x1, waiting for transfers between devices, body(): made = lax.all_gather(made, 'ctx', axis=0, tiled=False)  101 us
    all_to_all x1, blocking collectives, body(): lax.all_to_all(mine, 'shard', split_axis=0, concat_axis=0, tiled=True)  85.4 us
    all_gather x1, blocking collectives, body(): lax.all_gather(b_qkv, 'shard', axis=0, tiled=True)  80.1 us
    unnamed x98, local copies, waits for them, and re-layouts  75.6 us
    all_gather x1, waiting for transfers between devices, body(): grad_all = lax.all_gather(my_half(grad_rows), everyone, axis=0, tiled=True)  42 us
    unnamed x15, waiting for transfers between devices  40.7 us
  transfers between devices with their start and end apart: 16, of which 11 were waited for; matrix products, arithmetic and copies ran while one was open for 9% of the time, Pallas kernels for 0%

profile of v1, /device:TPU:0, one launch (start us, length us, event | category | flops | bytes accessed | tf_op | source)
XLA Modules:
  0.0 1073.5 jit_solution(9779028314949828245)
XLA Ops:
  12.9 37.7 %all-gather.2 = bf16[4,1,384]{2,1,0:T(2,128)(2,1)S(1)} all-gather(bf16[1,1,384]{2,1,0:T(2,128)(2,1)S(1)} %reshape.570), channel_id=1, replica_groups=mesh['shard'=4,'ctx'=4,'tp'=2] {'shard'}, dimensions={0}, use_global_device_ids=true | all-gather | bytes 3840 | tf_op jit(solution)/shard_map/all_gather | solution.py:108
  51.6 80.1 %all_gather.35 = bf16[128,1,8]{2,1,0:T(2,128)(2,1)S(1)} all-gather(bf16[32,1,8]{2,1,0:T(2,128)(2,1)S(1)} %copy.68), channel_id=1, replica_groups=mesh['shard'=4,'ctx'=4,'tp'=2] {'shard'}, dimensions={0}, use_global_device_ids=true | all-gather | bytes 2560 | tf_op jit(solution)/shard_map/all_gather | solution.py:109
  139.7 9.0 all_gather.36
  157.1 11.9 %all-gather.3 = bf16[4,1,384]{2,1,0:T(2,128)(2,1)S(1)} all-gather(bf16[1,1,384]{2,1,0:T(2,128)(2,1)S(1)} %reshape.572), channel_id=1, replica_groups=mesh['shard'=4,'ctx'=4,'tp'=2] {'shard'}, dimensions={0}, use_global_device_ids=true | all-gather | bytes 3840 | tf_op jit(solution)/shard_map/all_gather | solution.py:110
  186.5 18.0 %copy.72 = bf16[384,2,4480]{0,2,1:T(8,128)(2,1)} copy(bf16[384,2,4480]{2,1,0:T(2,128)(2,1)} %param.17) | data formatting | bytes 13762560 | tf_op args[7]
  207.9 85.4 %all_to_all.10 = bf16[4,384,3,280]{1,3,2,0:T(8,128)(2,1)S(1)} all-to-all(bf16[4,384,3,280]{1,3,2,0:T(8,128)(2,1)S(1)} %copy.74), channel_id=1, replica_groups=mesh['shard'=4,'ctx'=4,'tp'=2] {'shard'}, dimensions={0} | all-to-all | bytes 5160960 | tf_op jit(solution)/shard_map/all_to_all | solution.py:126
  296.4 9.2 fusion.93
  305.6 42.0 %all-gather.13.cloned.1.call-done = bf16[1,2048,1536]{2,1,0:T(8,128)(2,1)} async-done(((bf16[1,64,1536]{2,1,0:T(8,128)(2,1)}), bf16[1,2048,1536]{2,1,0:T(8,128)(2,1)}) %all-gather.13.cloned.1.call-update) | async-done | bytes 6291472 | tf_op jit(solution)/shard_map/all_gather | solution.py:131
  374.4 103.4 %reduce-scatter.13.cloned.1.call-done = bf16[64,1536]{1,0:T(8,128)(2,1)} async-done(((bf16[2048,1536]{1,0:T(8,128)(2,1)}), bf16[64,1536]{1,0:T(8,128)(2,1)}) %reduce-scatter.13.cloned.1.call-update) | async-done | bytes 196624 | tf_op jit(solution)/shard_map/reduce_scatter | solution.py:190
  481.6 116.3 %reduce-scatter.11.cloned.1.call-done = bf16[64,1536]{1,0:T(8,128)(2,1)} async-done(((bf16[2048,1536]{1,0:T(8,128)(2,1)}), bf16[64,1536]{1,0:T(8,128)(2,1)}) %reduce-scatter.11.cloned.1.call-update) | async-done | bytes 196624 | tf_op jit(solution)/shard_map/reduce_scatter | solution.py:190
  609.9 20.2 %reduce-scatter.19.cloned.1.call-done = bf16[128,256]{1,0:T(8,128)(2,1)} async-done(((bf16[512,256]{1,0:T(8,128)(2,1)}), bf16[128,256]{1,0:T(8,128)(2,1)}) %reduce-scatter.19.cloned.1.call-update) | async-done | bytes 65552
  656.7 48.0 %reduce-scatter.17.cloned.1.call-done = bf16[384,768]{1,0:T(8,128)(2,1)} async-done(((bf16[1536,768]{1,0:T(8,128)(2,1)}), bf16[384,768]{1,0:T(8,128)(2,1)}) %reduce-scatter.17.cloned.1.call-update) | async-done | bytes 589840 | tf_op jit(solution)/shard_map/reduce_scatter | solution.py:240
  704.7 81.7 %reduce-scatter.15.cloned.1.call-done = bf16[384,1,8,128]{3,0,2,1:T(8,128)(2,1)} async-done(((bf16[1536,1,8,128]{3,0,2,1:T(8,128)(2,1)}), bf16[384,1,8,128]{3,0,2,1:T(8,128)(2,1)}) %reduce-scatter.15.cloned.1.call-update) | async-done | bytes 786448 | tf_op jit(solution)/shard_map/reduce_scatter | solution.py:240
  788.4 19.6 %reduce-scatter.21.cloned.1.call-done = bf16[32,8]{1,0:T(8,128)(2,1)} async-done(((bf16[128,8]{1,0:T(8,128)(2,1)}), bf16[32,8]{1,0:T(8,128)(2,1)}) %reduce-scatter.21.cloned.1.call-update) | async-done | bytes 528
  808.8 19.3 %all-reduce.11.cloned.1.call-done = f32[128,1536]{1,0:T(8,128)} async-done(((f32[128,1536]{1,0:T(8,128)}), f32[128,1536]{1,0:T(8,128)}) %all-reduce.11.cloned.1.call-update) | async-done | bytes 786448 | tf_op jit(solution)/shard_map/psum | solution.py:72
  829.4 12.2 %all-reduce.4 = (bf16[1536]{0:T(1024)(128)(2,1)S(1)}, bf16[1536]{0:T(1024)(128)(2,1)S(1)}) all-reduce(bf16[1536]{0:T(1024)(128)(2,1)S(1)} %get-tuple-element.47, bf16[1536]{0:T(1024)(128)(2,1)S(1)} %copy-done.23), channel_id=7, replica_groups=mesh['shard'=4,'ctx'=4,'tp'=2] {'shard'}, use_global_device_ids=true, to_apply=%region_13.14.clone | all-reduce | flops 3072 | bytes 12288
  841.8 10.1 all-reduce.2
  856.0 34.0 %all-reduce.13.cloned.1.call-done = (bf16[384,1,8,128]{3,0,2,1:T(8,128)(2,1)}, bf16[384,768]{1,0:T(8,128)(2,1)}) async-done(((bf16[384,1,8,128]{3,0,2,1:T(8,128)(2,1)}, bf16[384,768]{1,0:T(8,128)(2,1)}), (bf16[384,1,8,128]{3,0,2,1:T(8,128)(2,1)}, bf16[384,768]{1,0:T(8,128)(2,1)})) %all-reduce.13.cloned.1.call-update) | async-done | bytes 1376272 | tf_op jit(solution)/shard_map/psum | solution.py:241
  894.5 100.9 %all-gather.15.cloned.1.call-done = bf16[16,384,840]{1,2,0:T(8,128)(2,1)} async-done(((bf16[4,384,840]{1,2,0:T(8,128)(2,1)}), bf16[16,384,840]{1,2,0:T(8,128)(2,1)}) %all-gather.15.cloned.1.call-update) | async-done | bytes 10321936 | tf_op jit(solution)/shard_map/all_gather | solution.py:201
  995.5 12.6 %convert_multiply_fusion = f32[16,384,840]{1,2,0:T(8,128)} fusion(bf16[16,384,840]{1,2,0:T(8,128)(2,1)} %all-gather.15.cloned.1.call-done), kind=kLoop, calls=%fused_computation.1 | loop fusion | flops 10321920 | bytes 30965760 | tf_op jit(solution)/shard_map/mul | solution.py:204
  1008.1 8.2 copy.84
  1026.4 10.7 slice.106
  1037.1 21.5 %copy.86 = f32[384,2,4480]{2,1,0:T(2,128)} copy(f32[384,2,4480]{0,2,1:T(8,128)} %slice.106) | data formatting | bytes 27525120
  1058.6 8.4 copy.87
  (214 shorter events, 137.8 us)
Async XLA Ops:
  7.2 43.5 %copy-start.33 = (s32[1,128]{1,0:T(1,128)S(1)}, s32[1,128]{1,0:T(1,128)}, u32[]{:S(2)}) copy-start(s32[1,128]{1,0:T(1,128)} %param.11) | copy-start | bytes 1540
  7.2 129.2 %all-gather.9.cloned.1.call-start = ((), (), s32[]{:S(2)}) async-start(), calls=%async_computation.8 | async-start | bytes 3932160 | tf_op jit(solution)/shard_map/all_gather | solution.py:106
  9.7 165.9 %all-reduce.9.cloned.1.call-start = ((), (), s32[]{:S(2)}) async-start(), calls=%async_computation.9 | async-start | bytes 1572864 | tf_op jit(solution)/shard_map/psum | solution.py:72
  9.8 40.9 %collective-permute-start = (bf16[1,384,768]{2,1,0:T(8,128)(2,1)S(1)}, bf16[1,384,768]{2,1,0:T(8,128)(2,1)S(1)}, u32[]{:S(2)}, u32[]{:S(2)}) collective-permute-start(bf16[1,384,768]{2,1,0:T(8,128)(2,1)S(1)} %bitcast.268), channel_id=1, source_target_pairs={{0,8},{8,0},{16,24},{24,16},{1,9},{9,1},{17,25},{25,17},{2,10},{10... | collective-permute-start | bytes 1769480 | tf_op jit(solution)/shard_map/ppermute | solution.py:23
  50.9 81.8 %copy-start.1 = (bf16[1,128,1536]{2,1,0:T(8,128)(2,1)S(1)}, bf16[1,128,1536]{2,1,0:T(8,128)(2,1)}, u32[]{:S(2)}) copy-start(bf16[1,128,1536]{2,1,0:T(8,128)(2,1)} %param.10) | copy-start | bytes 1179652
  51.1 83.3 %collective-permute-start.1 = (bf16[2,384,768]{2,1,0:T(8,128)(2,1)S(1)}, bf16[2,384,768]{2,1,0:T(8,128)(2,1)}, u32[]{:S(2)}, u32[]{:S(2)}) collective-permute-start(bf16[2,384,768]{2,1,0:T(8,128)(2,1)S(1)} %get-tuple-element.66), channel_id=1, source_target_pairs={{0,16},{8,24},{16,0},{24,8},{1,17},{9,25},{17,1},{25,9},{2,18},{10... | collective-permute-start | bytes 3538952 | tf_op jit(solution)/shard_map/ppermute | solution.py:23
  157.1 139.4 %all-gather.11.cloned.1.call-start = ((), (), s32[]{:S(2)}) async-start(), calls=%async_computation.10 | async-start | bytes 6488064 | tf_op jit(solution)/shard_map/all_gather | solution.py:178
  178.8 168.8 %all-gather.13.cloned.1.call-start = ((), (), s32[]{:S(2)}) async-start(), calls=%async_computation.16 | async-start | bytes 6488064 | tf_op jit(solution)/shard_map/all_gather | solution.py:131
  180.5 297.3 %reduce-scatter.13.cloned.1.call-start = ((), (), s32[]{:S(2)}) async-start(), calls=%async_computation.12 | async-start | bytes 6488064 | tf_op jit(solution)/shard_map/reduce_scatter | solution.py:190
  364.1 233.7 %reduce-scatter.11.cloned.1.call-start = ((), (), s32[]{:S(2)}) async-start(), calls=%async_computation.11 | async-start | bytes 6488064 | tf_op jit(solution)/shard_map/reduce_scatter | solution.py:190
  371.9 258.2 %reduce-scatter.19.cloned.1.call-start = ((), (), s32[]{:S(2)}) async-start(), calls=%async_computation.18 | async-start | bytes 327680
  374.4 225.9 %copy-start.11 = (bf16[1,128,1536]{2,1,0:T(8,128)(2,1)S(1)}, bf16[1,128,1536]{2,1,0:T(8,128)(2,1)}, u32[]{:S(2)}) copy-start(bf16[1,128,1536]{2,1,0:T(8,128)(2,1)} %param.19) | copy-start | bytes 1179652
  374.4 225.9 %copy-start.29 = (f32[128]{0:T(128)S(1)}, f32[128]{0:T(128)}, u32[]{:S(2)}) copy-start(f32[128]{0:T(128)} %copy-done.28) | copy-start | bytes 1540
  374.4 225.9 %copy-start.34 = (f32[128]{0:T(128)S(1)}, f32[128]{0:T(128)}, u32[]{:S(2)}) copy-start(f32[128]{0:T(128)} %get-tuple-element.83) | copy-start | bytes 1540
  481.6 120.0 %copy-start.6 = (bf16[6,128,128]{1,2,0:T(8,128)(2,1)S(1)}, bf16[6,128,128]{1,2,0:T(8,128)(2,1)}, u32[]{:S(2)}) copy-start(bf16[6,128,128]{1,2,0:T(8,128)(2,1)} %copy-done.5) | copy-start | bytes 589828
  606.6 98.0 %reduce-scatter.17.cloned.1.call-start = ((), (), s32[]{:S(2)}) async-start(), calls=%async_computation.15 | async-start | bytes 2949120 | tf_op jit(solution)/shard_map/reduce_scatter | solution.py:240
  608.9 177.5 %reduce-scatter.15.cloned.1.call-start = ((), (), s32[]{:S(2)}) async-start(), calls=%async_computation.14 | async-start | bytes 3932160 | tf_op jit(solution)/shard_map/reduce_scatter | solution.py:240
  647.6 138.9 %all-to-all-start.1 = ((bf16[4,384,840]{1,2,0:T(8,128)(2,1)}), bf16[4,384,840]{1,2,0:T(8,128)(2,1)}, u32[]{:S(2)}, u32[]{:S(2)}) async-start(bf16[4,384,840]{1,2,0:T(8,128)(2,1)} %bitcast.250), calls=%async_computation.5 | async-start | bytes 5160960 | tf_op jit(solution)/shard_map/all_to_all | solution.py:200
  652.2 155.8 %reduce-scatter.21.cloned.1.call-start = ((), (), s32[]{:S(2)}) async-start(), calls=%async_computation.19 | async-start | bytes 40960
  653.2 174.9 %all-reduce.11.cloned.1.call-start = ((), (), s32[]{:S(2)}) async-start(), calls=%async_computation.13 | async-start | bytes 1572864 | tf_op jit(solution)/shard_map/psum | solution.py:72
  656.6 130.5 %copy-start.36 = (u32[32]{0:T(128)S(1)}, u32[32]{0:T(128)}, u32[]{:S(2)}) copy-start(u32[32]{0:T(128)} %constant.67) | copy-start | bytes 388
  656.7 233.3 %all-reduce.13.cloned.1.call-start = ((), (), s32[]{:S(2)}) async-start(), calls=%async_computation.20 | async-start | bytes 2752512 | tf_op jit(solution)/shard_map/psum | solution.py:241
  786.4 67.2 %copy-start.35 = (f32[128]{0:T(128)S(1)}, f32[128]{0:T(128)}, u32[]{:S(2)}) copy-start(f32[128]{0:T(128)} %get-tuple-element.81) | copy-start | bytes 1540
  786.4 209.0 %all-gather.15.cloned.1.call-start = ((), (), s32[]{:S(2)}) async-start(), calls=%async_computation.17 | async-start | bytes 12902400 | tf_op jit(solution)/shard_map/all_gather | solution.py:201
  (33 other events, 226.0 us)
Sparse Core Ops, SparseCore 0:
  10.2 104.1 all-gather.8
  157.2 18.3 all-reduce.8
  179.1 96.6 all-gather.10
  279.1 68.5 all-gather.12
  364.3 113.4 reduce-scatter.12
  483.9 113.9 reduce-scatter.10
  606.8 23.3 reduce-scatter.18
  632.4 72.2 reduce-scatter.16
  707.6 78.7 reduce-scatter.14
  789.1 18.9 reduce-scatter.20
  810.9 17.1 all-reduce.10
  831.1 58.9 all-reduce.12
  891.9 103.5 all-gather.14
